TPU v7x, 16 devices: a whole 2x2x2 slice. The times are simulated.
16 devices in a mesh: ep: 16 (over z, y, x, core).
Axes of the slice: x: 2, y: 2, z: 2, core: 2. Of those that a mesh axis runs over, the one named last changes fastest.
Arguments:
- tokens: bfloat16 [256, 256, 768], P('ep')
- pad_mask: int32 [256, 256], P('ep')
- second_draw: float32 [256, 256], P('ep')
- choices: int32 [256, 256, 2], P('ep')
- norm_attn: float32 [768], replicated
- w_query: bfloat16 [768, 12, 64], replicated
- w_key: bfloat16 [768, 12, 64], replicated
- w_value: bfloat16 [768, 12, 64], replicated
- w_attn_out: bfloat16 [12, 64, 768], replicated
- norm_moe: float32 [768], replicated
- w_gate: float32 [768, 128], replicated
- w_in: bfloat16 [128, 768, 3072], P('ep')
- w_out: bfloat16 [128, 3072, 768], P('ep')
Outputs:
- output 1: bfloat16 [256, 256, 768], P('ep')
- output 2: float32 [], replicated
All inputs are finite; a program needn't handle non-finite values.
Results may differ from a plain program's by a relative error of at most 0.0175475.
Values are sent between devices in bfloat16 or wider.
A program may use at most 1 GiB of HBM per device.

v0:
```python
import jax
import jax.numpy as jnp
from jax import lax
from jax.sharding import PartitionSpec as P, NamedSharding

NORM_EPS = 1e-6


def rms_norm(values, scale_vec):
    values_f = values.astype(jnp.float32)
    inv_rms = lax.rsqrt(jnp.mean(values_f * values_f, axis=-1, keepdims=True) + NORM_EPS)
    return (values_f * inv_rms * scale_vec).astype(jnp.bfloat16)


def attention_block(tokens, pad_mask, norm_attn, w_query, w_key, w_value, w_attn_out):
    normed = rms_norm(tokens, norm_attn)
    q_heads = jnp.einsum("gsd,dhc->gshc", normed, w_query, preferred_element_type=jnp.float32).astype(jnp.bfloat16)
    k_heads = jnp.einsum("gsd,dhc->gshc", normed, w_key, preferred_element_type=jnp.float32).astype(jnp.bfloat16)
    v_heads = jnp.einsum("gsd,dhc->gshc", normed, w_value, preferred_element_type=jnp.float32).astype(jnp.bfloat16)
    head_scale = q_heads.shape[-1] ** -0.5
    scores = jnp.einsum("gqhc,gkhc->ghqk", q_heads, k_heads, preferred_element_type=jnp.float32) * head_scale
    scores = jnp.where(pad_mask[:, None, None, :] == 1, scores, -1e30)
    attn_probs = jax.nn.softmax(scores, axis=-1).astype(jnp.bfloat16)
    context = jnp.einsum("ghqk,gkhc->gqhc", attn_probs, v_heads, preferred_element_type=jnp.float32).astype(jnp.bfloat16)
    attn_out = jnp.einsum("gqhc,hcd->gqd", context, w_attn_out, preferred_element_type=jnp.float32)
    return (tokens.astype(jnp.float32) + attn_out).astype(jnp.bfloat16)


def gate_tokens(moe_in, pad_mask, second_draw, choices, w_gate, capacity):
    seq_len = moe_in.shape[1]
    expert_ids = jnp.arange(w_gate.shape[1])
    logits = jnp.einsum("gsd,de->gse", moe_in, w_gate, precision=lax.Precision.HIGHEST, preferred_element_type=jnp.float32)
    gate_probs = jax.nn.softmax(logits, axis=-1)
    is_valid = pad_mask == 1
    first_hot = choices[:, :, 0:1] == expert_ids
    second_hot = choices[:, :, 1:2] == expert_ids
    p_first = jnp.sum(jnp.where(first_hot, gate_probs, 0.0), axis=-1)
    p_second = jnp.sum(jnp.where(second_hot, gate_probs, 0.0), axis=-1)
    gate_first = p_first / (p_first + p_second)
    gate_second = p_second / (p_first + p_second)
    want_second = is_valid & (second_draw < 2.0 * gate_second)
    first_take = (first_hot & is_valid[:, :, None]).astype(jnp.int32)
    first_pos = jnp.sum((jnp.cumsum(first_take, axis=1) - 1) * first_take, axis=-1)
    first_count = jnp.sum(first_take, axis=1)
    keep_first = is_valid & (first_pos < capacity)
    second_take = (second_hot & want_second[:, :, None]).astype(jnp.int32)
    second_pos = jnp.sum((jnp.cumsum(second_take, axis=1) - 1 + jnp.minimum(first_count, capacity)[:, None, :]) * second_take, axis=-1)
    keep_second = want_second & (second_pos < capacity)
    density = jnp.sum(jnp.where(is_valid[:, :, None], gate_probs, 0.0), axis=1) / seq_len
    aux_sum = jnp.sum(first_count.astype(jnp.float32) / seq_len * density)
    return gate_first, gate_second, first_pos, second_pos, keep_first, keep_second, aux_sum


def build_tensors(choices, gate_first, gate_second, first_pos, second_pos, keep_first, keep_second, experts, capacity):
    expert_ids = jnp.arange(experts)
    slot_ids = jnp.arange(capacity)
    first_slot = (first_pos[:, :, None] == slot_ids) & keep_first[:, :, None]
    second_slot = (second_pos[:, :, None] == slot_ids) & keep_second[:, :, None]
    first_mask = (choices[:, :, 0:1] == expert_ids)[:, :, :, None] & first_slot[:, :, None, :]
    second_mask = (choices[:, :, 1:2] == expert_ids)[:, :, :, None] & second_slot[:, :, None, :]
    dispatch = (first_mask | second_mask).astype(jnp.bfloat16)
    combine = (jnp.where(first_mask, gate_first[:, :, None, None], 0.0) + jnp.where(second_mask, gate_second[:, :, None, None], 0.0)).astype(jnp.bfloat16)
    return dispatch, combine


def solution(mesh):
    n_dev = mesh.shape["ep"]

    def local_step(tokens, pad_mask, second_draw, choices, norm_attn, w_query, w_key, w_value, w_attn_out, norm_moe, w_gate, w_in, w_out):
        groups_local = tokens.shape[0]
        seq_len = tokens.shape[1]
        experts = w_gate.shape[1]
        capacity = (2 * seq_len + experts - 1) // experts
        hidden = attention_block(tokens, pad_mask, norm_attn, w_query, w_key, w_value, w_attn_out)
        moe_in = rms_norm(hidden, norm_moe)
        gate_first, gate_second, first_pos, second_pos, keep_first, keep_second, aux_sum = gate_tokens(moe_in, pad_mask, second_draw, choices, w_gate, capacity)
        dispatch, combine = build_tensors(choices, gate_first, gate_second, first_pos, second_pos, keep_first, keep_second, experts, capacity)
        send_buf = jnp.einsum("gsec,gsd->egcd", dispatch, moe_in, preferred_element_type=jnp.float32).astype(jnp.bfloat16)
        received = lax.all_to_all(send_buf, "ep", 0, 1, tiled=True)
        inner_act = jnp.maximum(jnp.einsum("egcd,edf->egcf", received, w_in, preferred_element_type=jnp.float32), 0.0).astype(jnp.bfloat16)
        expert_out = jnp.einsum("egcf,efd->egcd", inner_act, w_out, preferred_element_type=jnp.float32).astype(jnp.bfloat16)
        returned = lax.all_to_all(expert_out, "ep", 1, 0, tiled=True)
        moe_out = jnp.einsum("gsec,egcd->gsd", combine, returned, preferred_element_type=jnp.float32)
        out_tokens = (hidden.astype(jnp.float32) + moe_out).astype(jnp.bfloat16)
        aux_loss = lax.psum(aux_sum, "ep") * experts / (groups_local * n_dev)
        return out_tokens, aux_loss

    by_group = P("ep")
    replicated = P()
    in_specs = (by_group, by_group, by_group, by_group, replicated, replicated, replicated, replicated, replicated, replicated, replicated, by_group, by_group)
    return jax.shard_map(local_step, mesh=mesh, in_specs=in_specs, out_specs=(by_group, replicated), check_vma=False)
```

profile of v0, /device:TPU:1, one launch (start us, length us, event | category | flops | bytes accessed | tf_op | source)
XLA Modules:
  0.0 656.2 jit_solution(3865602998437984180)
XLA Ops:
  0.6 0.0 copy-start
  0.7 1.0 fusion.111
  1.6 0.8 copy.67
  2.4 0.8 copy.71
  3.1 0.7 broadcast_compare_fusion
  3.9 4.1 fusion.13
  8.0 0.7 copy.68
  8.7 26.5 %fusion.41 = f32[16,12,256,256]{2,3,1,0:T(8,128)} fusion(bf16[16,256,768]{2,1,0:T(8,128)(2,1)} %param.13, f32[768]{0:T(1024)S(1)} %copy-done.9, f32[16,256]{1,0:T(8,128)S(1)} %add_rsqrt_fusion.1, bf16[768,12,64]{0,2,1:T(8,128)(2,1)S(1)} %copy-done, bf16[768,12,64]{0,2,1:T(8,128)(2,1)S(1)} %copy-done.2), kind=kOutput, calls=%fused_computation.47 | convolution fusion | flops 11305746432 | bytes 59001856 | tf_op jit(solution)/shard_map/gqhc,gkhc->ghqk/dot_general | solution.py:21
  35.2 50.5 %fusion.112 = (f32[16,12,256]{2,1,0:T(8,128)S(1)}, f32[16,12,256,256]{2,3,1,0:T(8,128)}) fusion(f32[16,12,256,256]{2,3,1,0:T(8,128)} %fusion.41, pred[16,256]{1,0:T(8,128)(4,1)S(1)} %broadcast_compare_fusion), kind=kOutput, calls=%fused_computation.124 | output fusion | flops 75497728 | bytes 100864000 | tf_op jit(solution)/shard_map/sub | solution.py:23
  85.7 0.0 copy-done.25
  85.7 9.1 %fusion.88 = bf16[16,256,12,64]{1,3,2,0:T(8,128)(2,1)} fusion(bf16[16,256,768]{2,1,0:T(8,128)(2,1)} %param.13, f32[768]{0:T(1024)S(1)} %copy-done.9, f32[16,256]{1,0:T(8,128)S(1)} %add_rsqrt_fusion.1, bf16[768,12,64]{0,2,1:T(8,128)(2,1)S(1)} %copy-done.25), kind=kOutput, calls=%fused_computation.87 | convolution fusion | flops 4844421120 | bytes 13782016 | tf_op jit(solution)/shard_map/gsd,dhc->gshc/dot_general | solution.py:19
  94.8 0.0 copy-done.26
  94.8 24.9 %fusion.17 = (f32[16,256]{1,0:T(8,128)S(1)}, bf16[16,256,768]{2,1,0:T(8,128)(2,1)}) fusion(bf16[12,64,768]{2,1,0:T(8,128)(2,1)S(1)} %copy-done.26, f32[16,12,256,256]{2,3,1,0:T(8,128)} %get-tuple-element.13, f32[16,12,256]{2,1,0:T(8,128)S(1)} %get-tuple-element.12, bf16[16,256,12,64]{1,3,2,0:T(8,128)(2,1)} %fusion.88, bf16[16,256,768]{2,1,0:T(8,128)(2,1)} %param.13), kind=kOutput, calls=%fused_computation.27 | convolution fusion | flops 6489632768 | bytes 70598656 | tf_op jit(solution)/shard_map/gqhc,hcd->gqd/dot_general | solution.py:25
  119.7 0.3 iota_compare_fusion.3
  120.1 0.3 iota_compare_fusion.1
  120.4 10.5 %fusion.46 = f32[16,256,128]{1,2,0:T(8,128)} fusion(bf16[16,256,768]{2,1,0:T(8,128)(2,1)} %get-tuple-element.15, f32[768]{0:T(1024)S(1)} %copy-done.28, f32[16,256]{1,0:T(8,128)S(1)} %add_rsqrt_fusion, f32[768,128]{1,0:T(8,128)S(1)} %copy-done.27), kind=kOutput, calls=%fused_computation.51 | convolution fusion | flops 4844421120 | bytes 8801280 | tf_op jit(solution)/shard_map/gsd,de->gse/dot_general | solution.py:32
  130.9 4.2 select_reduce_fusion
  135.1 0.0 copy-done.4
  135.1 0.0 copy-start.17
  135.1 0.0 copy-start.22
  135.2 1.3 fusion.74
  136.5 1.5 add_add_fusion.1
  137.9 1.9 copy.69
  139.9 0.6 fusion.71
  140.5 0.6 fusion.105
  141.2 0.1 copy.72
  141.3 1.3 fusion.72
  142.6 1.5 add_add_fusion
  144.1 1.9 copy.73
  146.0 0.7 fusion.70
  146.8 1.0 copy.43
  147.8 1.0 copy.49
  148.7 0.0 copy-start.7
  148.7 12.8 %convert_bitcast_fusion = bf16[128,16,4,768]{0,3,2,1:T(8,128)(2,1)} fusion(bf16[16,256,768]{2,1,0:T(8,128)(2,1)} %get-tuple-element.15, f32[768]{0:T(1024)S(1)} %copy-done.28, f32[16,256]{1,0:T(8,128)S(1)} %add_rsqrt_fusion, pred[16,256,4]{1,2,0:T(4,128)(4,1)S(1)} %fusion.102, pred[16,256,128]{2,1,0:T(8,128)(4,1)S(1)} %copy.49, ...), kind=kOutput, calls=%fused_computation.34 | convolution fusion | flops 3246391296 | bytes 19975168 | tf_op jit(solution)/shard_map/gsec,gsd->egcd/dot_general | solution.py:78
  161.6 21.4 %copy.54 = bf16[128,16,4,768]{3,2,1,0:T(4,128)(2,1)} copy(bf16[128,16,4,768]{0,3,2,1:T(8,128)(2,1)} %convert_bitcast_fusion) | data formatting | bytes 25165824 | tf_op jit(solution)/shard_map/convert_element_type | solution.py:78
  183.0 147.4 %all_to_all.36 = bf16[128,16,4,768]{3,2,1,0:T(4,128)(2,1)S(1)} all-to-all(bf16[128,16,4,768]{3,2,1,0:T(4,128)(2,1)} %copy.54), channel_id=1, replica_groups=mesh['ep'=16] {'ep'}, dimensions={0} | all-to-all | bytes 25165824 | tf_op jit(solution)/shard_map/all_to_all | solution.py:79
  330.4 3.0 copy.55
  333.4 5.8 copy.56
  339.2 49.1 %maximum_convert_fusion.6 = bf16[8,256,4,3072]{3,1,2,0:T(8,128)(2,1)} fusion(bf16[8,256,4,768]{3,1,2,0:T(8,128)(2,1)} %bitcast.113, bf16[8,768,3072]{2,1,0:T(8,128)(2,1)} %param.24), kind=kOutput, calls=%fused_computation.3.clone.clone.clone.clone.1 | convolution fusion | flops 38705037312 | bytes 100663296 | tf_op jit(solution)/shard_map/egcd,edf->egcf/dot_general | solution.py:80
  388.4 48.4 %fusion.31 = bf16[8,256,4,768]{3,1,2,0:T(8,128)(2,1)} fusion(bf16[8,3072,768]{2,1,0:T(8,128)(2,1)} %param.25, bf16[8,256,4,3072]{3,1,2,0:T(8,128)(2,1)} %maximum_convert_fusion.6), kind=kOutput, calls=%fused_computation.41 | convolution fusion | flops 38660997120 | bytes 100663296 | tf_op jit(solution)/shard_map/egcf,efd->egcd/dot_general | solution.py:81
  436.8 17.6 %copy.57 = bf16[8,256,4,768]{3,2,0,1:T(4,128)(2,1)} copy(bf16[8,256,4,768]{3,1,2,0:T(8,128)(2,1)} %fusion.31) | data formatting | bytes 25165824 | tf_op jit(solution)/shard_map/convert_element_type | solution.py:81
  454.4 0.0 copy-start.8
  454.4 6.5 all-to-all-start.1
  461.0 0.6 multiply_reduce_fusion
  461.6 181.0 %psum.7 = f32[]{:T(128)} all-reduce(f32[]{:T(128)} %multiply_reduce_fusion), channel_id=1, replica_groups=mesh['ep'=16] {'ep'}, use_global_device_ids=true, to_apply=%region_17.18 | all-reduce | flops 1 | bytes 8 | tf_op jit(solution)/shard_map/psum | solution.py:85
  643.3 0.0 all-to-all-done.1
  643.3 0.0 copy-start.1
  643.3 11.3 %fusion.20 = bf16[16,256,768]{2,1,0:T(8,128)(2,1)} fusion(bf16[16,256,768]{2,1,0:T(8,128)(2,1)} %get-tuple-element.15, bf16[8,16,16,4,768]{4,3,0,2,1:T(4,128)(2,1)} %bitcast.32, f32[16,256]{1,0:T(8,128)S(1)} %copy-done.23, f32[16,256]{1,0:T(8,128)S(1)} %add_divide_fusion.1, pred[16,256,4]{1,2,0:T(4,128)(4,1)S(1)} %copy-done.21, ...), kind=kOutput, calls=%fused_computation.30 | convolution fusion | flops 3243245568 | bytes 26279936 | tf_op jit(solution)/shard_map/gsec,egcd->gsd/dot_general | solution.py:83
  (61 shorter events, 0.2 us)
Async XLA Ops:
  0.6 8.0 %copy-start = (bf16[768,12,64]{0,2,1:T(8,128)(2,1)S(1)}, bf16[768,12,64]{0,2,1:T(8,128)(2,1)}, u32[]{:S(2)}) copy-start(bf16[768,12,64]{0,2,1:T(8,128)(2,1)} %param.19) | copy-start | bytes 3538948
  0.6 8.0 %copy-start.9 = (f32[768]{0:T(1024)S(1)}, f32[768]{0:T(1024)}, u32[]{:S(2)}) copy-start(f32[768]{0:T(1024)} %param.17) | copy-start | bytes 9220
  0.7 8.0 %copy-start.2 = (bf16[768,12,64]{0,2,1:T(8,128)(2,1)S(1)}, bf16[768,12,64]{0,2,1:T(8,128)(2,1)}, u32[]{:S(2)}) copy-start(bf16[768,12,64]{0,2,1:T(8,128)(2,1)} %param.18) | copy-start | bytes 3538948
  35.2 50.5 %copy-start.25 = (bf16[768,12,64]{0,2,1:T(8,128)(2,1)S(1)}, bf16[768,12,64]{0,2,1:T(8,128)(2,1)}, u32[]{:S(2)}) copy-start(bf16[768,12,64]{0,2,1:T(8,128)(2,1)} %param.20) | copy-start | bytes 3538948
  85.7 9.1 %copy-start.26 = (bf16[12,64,768]{2,1,0:T(8,128)(2,1)S(1)}, bf16[12,64,768]{2,1,0:T(8,128)(2,1)}, u32[]{:S(2)}) copy-start(bf16[12,64,768]{2,1,0:T(8,128)(2,1)} %param.21) | copy-start | bytes 3538948
  94.8 25.6 %copy-start.27 = (f32[768,128]{1,0:T(8,128)S(1)}, f32[768,128]{1,0:T(8,128)}, u32[]{:S(2)}) copy-start(f32[768,128]{1,0:T(8,128)} %param.23) | copy-start | bytes 1179652
  94.8 25.6 %copy-start.28 = (f32[768]{0:T(1024)S(1)}, f32[768]{0:T(1024)}, u32[]{:S(2)}) copy-start(f32[768]{0:T(1024)} %param.22) | copy-start | bytes 9220
  130.9 4.2 copy-start.4
  130.9 4.2 copy-start.10
  135.1 5.4 copy-start.13
  135.1 5.4 copy-start.15
  135.1 5.4 copy-start.17
  135.1 5.4 copy-start.22
  135.2 6.1 copy-start.3
  140.5 6.2 copy-start.11
  141.2 7.6 %copy-start.18 = (pred[16,256,4]{1,2,0:T(4,128)(4,1)}, pred[16,256,4]{1,2,0:T(4,128)(4,1)S(1)}, u32[]{:S(2)}) copy-start(pred[16,256,4]{1,2,0:T(4,128)(4,1)S(1)} %fusion.101) | copy-start | bytes 49156
  146.8 14.8 %copy-start.20 = (pred[16,256,4]{1,2,0:T(4,128)(4,1)}, pred[16,256,4]{1,2,0:T(4,128)(4,1)S(1)}, u32[]{:S(2)}) copy-start(pred[16,256,4]{1,2,0:T(4,128)(4,1)S(1)} %fusion.102) | copy-start | bytes 49156
  147.7 13.8 %copy-start.5 = (pred[16,256,128]{2,1,0:T(8,128)(4,1)}, pred[16,256,128]{2,1,0:T(8,128)(4,1)S(1)}, u32[]{:S(2)}) copy-start(pred[16,256,128]{2,1,0:T(8,128)(4,1)S(1)} %copy.43) | copy-start | bytes 1572868
  148.7 12.8 %copy-start.7 = (pred[16,256,128]{2,1,0:T(8,128)(4,1)}, pred[16,256,128]{2,1,0:T(8,128)(4,1)S(1)}, u32[]{:S(2)}) copy-start(pred[16,256,128]{2,1,0:T(8,128)(4,1)S(1)} %copy.49) | copy-start | bytes 1572868
  454.4 6.6 %copy-start.12 = (s32[16,128]{1,0:T(8,128)S(1)}, s32[16,128]{1,0:T(8,128)}, u32[]{:S(2)}) copy-start(s32[16,128]{1,0:T(8,128)} %copy-done.11) | copy-start | bytes 24580
  454.4 6.6 %copy-start.24 = (f32[16,128]{1,0:T(8,128)S(1)}, f32[16,128]{1,0:T(8,128)}, u32[]{:S(2)}) copy-start(f32[16,128]{1,0:T(8,128)} %get-tuple-element.2) | copy-start | bytes 24580
  454.4 188.9 %copy-start.14 = (f32[16,256]{1,0:T(8,128)S(1)}, f32[16,256]{1,0:T(8,128)}, u32[]{:S(2)}) copy-start(f32[16,256]{1,0:T(8,128)} %copy-done.13) | copy-start | bytes 49156
  454.4 188.9 %copy-start.16 = (f32[16,256]{1,0:T(8,128)S(1)}, f32[16,256]{1,0:T(8,128)}, u32[]{:S(2)}) copy-start(f32[16,256]{1,0:T(8,128)} %copy-done.15) | copy-start | bytes 49156
  454.4 188.9 %copy-start.6 = (pred[16,256,128]{2,1,0:T(8,128)(4,1)S(1)}, pred[16,256,128]{2,1,0:T(8,128)(4,1)}, u32[]{:S(2)}) copy-start(pred[16,256,128]{2,1,0:T(8,128)(4,1)} %copy-done.5) | copy-start | bytes 1572868
  454.4 188.9 %copy-start.8 = (pred[16,256,128]{2,1,0:T(8,128)(4,1)S(1)}, pred[16,256,128]{2,1,0:T(8,128)(4,1)}, u32[]{:S(2)}) copy-start(pred[16,256,128]{2,1,0:T(8,128)(4,1)} %copy-done.7) | copy-start | bytes 1572868
  454.4 188.9 %copy-start.19 = (pred[16,256,4]{1,2,0:T(4,128)(4,1)S(1)}, pred[16,256,4]{1,2,0:T(4,128)(4,1)}, u32[]{:S(2)}) copy-start(pred[16,256,4]{1,2,0:T(4,128)(4,1)} %copy-done.18) | copy-start | bytes 49156
  454.4 188.9 %copy-start.21 = (pred[16,256,4]{1,2,0:T(4,128)(4,1)S(1)}, pred[16,256,4]{1,2,0:T(4,128)(4,1)}, u32[]{:S(2)}) copy-start(pred[16,256,4]{1,2,0:T(4,128)(4,1)} %copy-done.20) | copy-start | bytes 49156
  454.4 188.9 %copy-start.23 = (f32[16,256]{1,0:T(8,128)S(1)}, f32[16,256]{1,0:T(8,128)}, u32[]{:S(2)}) copy-start(f32[16,256]{1,0:T(8,128)} %get-tuple-element.8) | copy-start | bytes 49156
  454.4 188.8 %all-to-all-start.1 = ((bf16[8,256,4,768]{3,2,0,1:T(4,128)(2,1)}), bf16[8,256,4,768]{3,2,0,1:T(4,128)(2,1)}, u32[]{:S(2)}, u32[]{:S(2)}) async-start(bf16[8,256,4,768]{3,2,0,1:T(4,128)(2,1)} %copy.57), calls=%async_computation.1 | async-start | bytes 25165824 | tf_op jit(solution)/shard_map/all_to_all | solution.py:82
  643.3 11.3 %copy-start.1 = (bf16[768,12,64]{0,2,1:T(8,128)(2,1)S(1)}, bf16[768,12,64]{0,2,1:T(8,128)(2,1)}, u32[]{:S(2)}) copy-start(bf16[768,12,64]{0,2,1:T(8,128)(2,1)} %param.19) | copy-start | bytes 3538948
where the time goes:
time: 668 us; the launch traced here: 656 us
  blocking collectives  328 us (49%)
  matrix products  193 us (29%)
  other arithmetic  68.1 us (10%)
  local copies, waits for them, and re-layouts  57 us (9%)
    psum x1, blocking collectives, local_step(): aux_loss = lax.psum(aux_sum, 'ep') * experts / (groups_local * n_dev)  181 us
    all_to_all x1, blocking collectives, local_step(): received = lax.all_to_all(send_buf, 'ep', 0, 1, tiled=True)  147 us
    sub x1, other arithmetic, attention_block(): attn_probs = jax.nn.softmax(scores, axis=-1).astype(jnp.bfloat16)  50.5 us
    dot_general x1, matrix products, local_step(): jnp.einsum('egcd,edf->egcf', received, w_in, preferred_element_type=jnp.f...  49.1 us
    dot_general x1, matrix products, local_step(): jnp.einsum('egcf,efd->egcd', inner_act, w_out, preferred_element_type=jnp...  48.4 us
    dot_general x1, matrix products, attention_block(): jnp.einsum('gqhc,gkhc->ghqk', q_heads, k_heads, preferred_element_type=jn...  26.5 us
    dot_general x1, matrix products, attention_block(): jnp.einsum('gqhc,hcd->gqd', context, w_attn_out, preferred_element_type=j...  24.9 us
    convert_element_type x1, local copies, waits for them, and re-layouts, local_step(): jnp.einsum('gsec,gsd->egcd', dispatch, moe_in, preferred_element_type=jnp...  21.4 us
  transfers between devices with their start and end apart: 1, of which 0 were waited for; matrix products, arithmetic and copies ran while one was open for 0% of the time, Pallas kernels for 0%

commit v1 on v0

v1 whole, which is shorter than its diff:
```python
import functools
import jax
import jax.numpy as jnp
from jax import lax
from jax.experimental import pallas as pl
from jax.experimental.pallas import tpu as pltpu
from jax.sharding import PartitionSpec as P

NORM_EPS = 1e-6
N_DEV = 16
MESH = pl.DeviceIdType.MESH
F32 = jnp.float32
BF16 = jnp.bfloat16
ORDER = (0, 9, 2, 11, 4, 13, 6, 15, 8, 1, 10, 3, 12, 5, 14, 7)
VMEM_LIMIT = 62 * 1024 * 1024


def partner(me, mask):
    out = 0
    for bit in range(4):
        val = lax.rem(me // (1 << bit), 2)
        out = out + (1 << bit) * ((1 - val) if (mask >> bit) & 1 else val)
    return out


def greet(me):
    barrier = pltpu.get_barrier_semaphore()
    for mask in range(1, N_DEV):
        pl.semaphore_signal(barrier, inc=1, device_id=(partner(me, mask),), device_id_type=MESH)


def rms_norm(values_f, scale_vec):
    inv_rms = lax.rsqrt(jnp.mean(values_f * values_f, axis=-1, keepdims=True) + NORM_EPS)
    return (values_f * inv_rms * scale_vec).astype(BF16)


def dot(a, b):
    return jnp.dot(a, b, preferred_element_type=F32)


def front_kernel(
    tokens_ref, keymask_ref, cols_ref, norm_attn_ref, wqkv_ref, wo_ref, norm_moe_ref, wgate_ref,
    hidden_ref, meta_ref, recv_ref, auxr_ref,
    qkv_s, ctx_s, wg_s, aux_s, send_s, send_sem, recv_sem, local_sem, aux_send_sem, aux_recv_sem,
    *, heads, head_dim, capacity,
):
    step = pl.program_id(0)
    steps = pl.num_programs(0)
    me = lax.axis_index("ep")
    seq = tokens_ref.shape[1]
    d_model = tokens_ref.shape[2]
    experts = wgate_ref.shape[1]
    e_loc = experts // N_DEV
    half = e_loc // 2
    slots = experts * capacity
    rows = 2 * capacity
    per_src = steps * rows

    def send_pair(pair):
        for place, mask in enumerate(ORDER):
            dev = partner(me, mask)
            src = send_s.at[pair, dev]
            dst = recv_ref.at[:, pl.ds(pl.multiple_of(place * per_src + pair * rows, rows), rows), :]
            if mask == 0:
                pltpu.make_async_copy(src, dst, local_sem.at[0]).start()
            else:
                pltpu.make_async_remote_copy(
                    src_ref=src, dst_ref=dst, send_sem=send_sem, recv_sem=recv_sem,
                    device_id=(dev,), device_id_type=MESH).start()

    @pl.when(step == 0)
    def _():
        greet(me)
        aux_s[...] = jnp.zeros_like(aux_s)
        wg = wgate_ref[...]
        hi = wg.astype(BF16)
        rest = wg - hi.astype(F32)
        mid = rest.astype(BF16)
        low = (rest - mid.astype(F32)).astype(BF16)
        wg_s[:, 0:experts] = hi
        wg_s[:, experts:2 * experts] = mid
        wg_s[:, 2 * experts:3 * experts] = low

    @pl.when(step == 1)
    def _():
        pl.semaphore_wait(pltpu.get_barrier_semaphore(), N_DEV - 1)

    @pl.when(step > 0)
    def _():
        send_pair(step - 1)

    x = tokens_ref[...].reshape(2 * seq, d_model)
    a = rms_norm(x.astype(F32), norm_attn_ref[...])
    qkv_s[...] = dot(a, wqkv_ref[...]).astype(BF16)

    width = 2 * head_dim
    lane = lax.broadcasted_iota(jnp.int32, (1, width), 1)
    ones = [(lane < head_dim).astype(F32).astype(BF16), (lane >= head_dim).astype(F32).astype(BF16)]
    scaled = [m * jnp.asarray(head_dim ** -0.5, BF16) for m in ones]
    hw = heads * head_dim
    for grp in range(2):
        tok = pl.ds(grp * seq, seq)
        keep_key = keymask_ref[grp] == 1
        for pair_idx in range(heads // 2):
            off = pair_idx * width
            q = qkv_s[tok, pl.ds(off, width)]
            k = qkv_s[tok, pl.ds(hw + off, width)]
            v = qkv_s[tok, pl.ds(2 * hw + off, width)]
            ctx = None
            for side in range(2):
                s = lax.dot_general(q * scaled[side], k, (((1,), (1,)), ((), ())), preferred_element_type=F32)
                s = jnp.where(keep_key, s, -1e30)
                ex = jnp.exp(s - jnp.max(s, axis=-1, keepdims=True))
                prob = (ex * (1.0 / jnp.sum(ex, axis=-1, keepdims=True))).astype(BF16)
                part = dot(prob, v * ones[side])
                ctx = part if ctx is None else ctx + part
            ctx_s[tok, pl.ds(off, width)] = ctx.astype(BF16)

    hidden = (x.astype(F32) + dot(ctx_s[...], wo_ref[...])).astype(BF16)
    hidden_ref[...] = hidden.reshape(2, seq, d_model)
    b = rms_norm(hidden.astype(F32), norm_moe_ref[...])
    lg = dot(b, wg_s[...])
    logits = (lg[:, 2 * experts:] + lg[:, experts:2 * experts]) + lg[:, :experts]
    ex = jnp.exp(logits - jnp.max(logits, axis=-1, keepdims=True))
    gate_probs = ex / jnp.sum(ex, axis=-1, keepdims=True)

    eid = lax.broadcasted_iota(jnp.int32, (seq, experts), 1)
    tri = (lax.broadcasted_iota(jnp.int32, (seq, seq), 0) >= lax.broadcasted_iota(jnp.int32, (seq, seq), 1)).astype(F32).astype(BF16)
    slot_id = lax.broadcasted_iota(jnp.int32, (seq, slots), 1)
    meta_lane = lax.broadcasted_iota(jnp.int32, (seq, experts), 1)
    picked = []
    for grp in range(2):
        p = gate_probs[grp * seq:(grp + 1) * seq]
        cols = cols_ref[grp]
        valid = cols[:, 0:1] == 1.0
        draw = cols[:, 1:2]
        e1 = cols[:, 2:3].astype(jnp.int32)
        e2 = cols[:, 3:4].astype(jnp.int32)
        hot1 = eid == e1
        hot2 = eid == e2
        p1 = jnp.sum(jnp.where(hot1, p, 0.0), axis=-1, keepdims=True)
        p2 = jnp.sum(jnp.where(hot2, p, 0.0), axis=-1, keepdims=True)
        g1 = p1 / (p1 + p2)
        g2 = p2 / (p1 + p2)
        want2 = valid & (draw < 2.0 * g2)
        take1 = jnp.where(hot1 & valid, 1.0, 0.0)
        take2 = jnp.where(hot2 & want2, 1.0, 0.0)
        cum = dot(tri, jnp.concatenate([take1, take2], axis=1).astype(BF16))
        cum1 = cum[:, :experts]
        cum2 = cum[:, experts:]
        count1 = cum1[seq - 1:seq, :]
        pos1 = jnp.sum((cum1 - 1.0) * take1, axis=-1, keepdims=True).astype(jnp.int32)
        pos2 = jnp.sum((cum2 - 1.0 + jnp.minimum(count1, float(capacity))) * take2, axis=-1, keepdims=True).astype(jnp.int32)
        keep1 = valid & (pos1 < capacity)
        keep2 = want2 & (pos2 < capacity)

        density = jnp.sum(jnp.where(valid, p, 0.0), axis=0, keepdims=True) / seq
        aux_s[0:1, :] += count1 / seq * density

        def places(e, pos, keep):
            dev = e // e_loc
            r = e - dev * e_loc
            upper = r // half
            i = r - upper * half
            side = upper if grp == 0 else 1 - upper
            disp = ((dev * half + i) * 2 + side) * capacity + pos
            comb = (e * 2 + side) * capacity + pos
            return jnp.where(keep, disp, -1), jnp.where(keep, comb, -1)

        d1, c1 = places(e1, pos1, keep1)
        d2, c2 = places(e2, pos2, keep2)
        meta = jnp.where(meta_lane == 0, c1.astype(F32), 0.0)
        meta = jnp.where(meta_lane == 1, c2.astype(F32), meta)
        meta = jnp.where(meta_lane == 2, g1, meta)
        meta = jnp.where(meta_lane == 3, g2, meta)
        meta_ref[grp] = meta
        disp_mat = jnp.where((slot_id == d1) | (slot_id == d2), 1.0, 0.0).astype(BF16)
        got = lax.dot_general(disp_mat, b[grp * seq:(grp + 1) * seq], (((0,), (0,)), ((), ())), preferred_element_type=F32)
        picked.append(got.reshape(N_DEV * half, rows, d_model))

    top = lax.broadcasted_iota(jnp.int32, (1, rows, 1), 1) < capacity
    lower = jnp.where(top, picked[0], picked[1]).astype(BF16)
    upper = jnp.where(top, picked[1], picked[0]).astype(BF16)
    send_s[step, :, 0:half] = lower.reshape(N_DEV, half, rows, d_model)
    send_s[step, :, half:e_loc] = upper.reshape(N_DEV, half, rows, d_model)

    @pl.when(step == steps - 1)
    def _():
        send_pair(steps - 1)
        for mask in range(1, N_DEV):
            pltpu.make_async_remote_copy(
                src_ref=aux_s, dst_ref=auxr_ref.at[mask], send_sem=aux_send_sem, recv_sem=aux_recv_sem,
                device_id=(partner(me, mask),), device_id_type=MESH).start()
        own = pltpu.make_async_copy(aux_s, auxr_ref.at[0], local_sem.at[1])
        own.start()
        own.wait()
        others = pl.ds(0, N_DEV - 1)
        pltpu.make_async_copy(send_s.at[:, others], send_s.at[:, others], send_sem).wait()
        pltpu.make_async_copy(send_s.at[:, 0], send_s.at[:, 0], local_sem.at[0]).wait()
        pltpu.make_async_copy(auxr_ref.at[others], auxr_ref.at[others], aux_send_sem).wait()
        pltpu.make_async_copy(auxr_ref.at[others], auxr_ref.at[others], aux_recv_sem).wait()
        arrived = recv_ref.at[:, pl.ds(0, (N_DEV - 1) * per_src), :]
        pltpu.make_async_copy(arrived, arrived, recv_sem).wait()


def expert_kernel(recv_ref, w_in_ref, w_out_ref, ret_ref, act_s, z_s, send_sem, recv_sem, local_sem, *, tile):
    e = pl.program_id(0)
    n_exp = pl.num_programs(0)
    me = lax.axis_index("ep")
    rows = recv_ref.shape[1]
    ff = w_in_ref.shape[2]
    per_src = rows // N_DEV
    n_tiles = rows // tile
    chunk = 1024

    @pl.when(e == 0)
    def _():
        greet(me)

    for t in range(n_tiles):
        x = recv_ref[0, pl.ds(t * tile, tile), :]
        for f in range(ff // chunk):
            act = dot(x, w_in_ref[0, :, pl.ds(f * chunk, chunk)])
            act_s[:, pl.ds(f * chunk, chunk)] = jnp.maximum(act, 0.0).astype(BF16)
        z_s[e, pl.ds(t * tile, tile), :] = dot(act_s[...], w_out_ref[0]).astype(BF16)

        if t == 0:
            @pl.when(e == 0)
            def _():
                pl.semaphore_wait(pltpu.get_barrier_semaphore(), N_DEV - 1)

        for place in range(t * tile // per_src, (t + 1) * tile // per_src):
            mask = ORDER[place]
            dev = partner(me, mask)
            src = z_s.at[e, pl.ds(place * per_src, per_src), :]
            dst = ret_ref.at[me * n_exp + e]
            if mask == 0:
                pltpu.make_async_copy(src, dst, local_sem).start()
            else:
                pltpu.make_async_remote_copy(
                    src_ref=src, dst_ref=dst, send_sem=send_sem, recv_sem=recv_sem,
                    device_id=(dev,), device_id_type=MESH).start()

    @pl.when(e == n_exp - 1)
    def _():
        sent = z_s.at[:, pl.ds(0, (N_DEV - 1) * per_src), :]
        pltpu.make_async_copy(sent, sent, send_sem).wait()
        own = z_s.at[:, pl.ds(0, per_src), :]
        pltpu.make_async_copy(own, own, local_sem).wait()
        arrived = ret_ref.at[pl.ds(0, (N_DEV - 1) * n_exp)]
        pltpu.make_async_copy(arrived, arrived, recv_sem).wait()


def back_kernel(ret_ref, hidden_ref, meta_ref, auxr_ref, out_ref, aux_ref, *, n_groups):
    experts, rows, d_model = ret_ref.shape
    seq = hidden_ref.shape[1]
    z = ret_ref[...].reshape(experts * rows, d_model)
    slot_id = lax.broadcasted_iota(jnp.int32, (seq, experts * rows), 1)
    for grp in range(2):
        meta = meta_ref[grp]
        c1 = meta[:, 0:1].astype(jnp.int32)
        c2 = meta[:, 1:2].astype(jnp.int32)
        comb = jnp.where(slot_id == c1, meta[:, 2:3], 0.0) + jnp.where(slot_id == c2, meta[:, 3:4], 0.0)
        moe = dot(comb.astype(BF16), z)
        out_ref[grp] = (hidden_ref[grp].astype(F32) + moe).astype(BF16)

    @pl.when(pl.program_id(0) == 0)
    def _():
        total = jnp.sum(auxr_ref[...], axis=0)
        total = jnp.sum(jnp.sum(total, axis=1, keepdims=True), axis=0, keepdims=True)
        aux_ref[...] = jnp.broadcast_to(total * (experts / n_groups), aux_ref.shape)


def solution(mesh):
    def local_step(tokens, pad_mask, second_draw, choices, norm_attn, w_query, w_key, w_value, w_attn_out, norm_moe, w_gate, w_in, w_out):
        groups, seq, d_model = tokens.shape
        _, heads, head_dim = w_query.shape
        experts = w_gate.shape[1]
        ff = w_in.shape[2]
        e_loc = experts // N_DEV
        capacity = (2 * seq + experts - 1) // experts
        hw = heads * head_dim
        rows = 2 * capacity
        steps = groups // 2
        all_rows = N_DEV * steps * rows

        wqkv = jnp.concatenate([w.reshape(d_model, hw) for w in (w_query, w_key, w_value)], axis=1)
        wo = w_attn_out.reshape(hw, d_model)
        cols = jnp.concatenate([
            pad_mask.astype(F32)[:, :, None], second_draw[:, :, None], choices.astype(F32)], axis=-1)
        keymask = pad_mask.reshape(groups, 1, seq)

        def whole(shape):
            return pl.BlockSpec(shape, lambda i: (0,) * len(shape), pipeline_mode=pl.Buffered(1))

        anywhere = pl.BlockSpec(memory_space=pl.ANY)
        hidden, meta, recv, auxr = pl.pallas_call(
            functools.partial(front_kernel, heads=heads, head_dim=head_dim, capacity=capacity),
            name="front",
            grid=(steps,),
            in_specs=[
                pl.BlockSpec((2, seq, d_model), lambda i: (i, 0, 0)),
                pl.BlockSpec((2, 1, seq), lambda i: (i, 0, 0)),
                pl.BlockSpec((2, seq, 4), lambda i: (i, 0, 0)),
                whole((1, d_model)), whole((d_model, 3 * hw)), whole((hw, d_model)),
                whole((1, d_model)), whole((d_model, experts)),
            ],
            out_specs=[
                pl.BlockSpec((2, seq, d_model), lambda i: (i, 0, 0)),
                pl.BlockSpec((2, seq, experts), lambda i: (i, 0, 0)),
                anywhere, anywhere,
            ],
            out_shape=[
                jax.ShapeDtypeStruct((groups, seq, d_model), BF16),
                jax.ShapeDtypeStruct((groups, seq, experts), F32),
                jax.ShapeDtypeStruct((e_loc, all_rows, d_model), BF16),
                jax.ShapeDtypeStruct((N_DEV, 8, experts), F32),
            ],
            scratch_shapes=[
                pltpu.VMEM((2 * seq, 3 * hw), BF16),
                pltpu.VMEM((2 * seq, hw), BF16),
                pltpu.VMEM((d_model, 3 * experts), BF16),
                pltpu.VMEM((8, experts), F32),
                pltpu.VMEM((steps, N_DEV, e_loc, rows, d_model), BF16),
                pltpu.SemaphoreType.DMA,
                pltpu.SemaphoreType.DMA,
                pltpu.SemaphoreType.DMA((2,)),
                pltpu.SemaphoreType.DMA,
                pltpu.SemaphoreType.DMA,
            ],
            compiler_params=pltpu.CompilerParams(
                dimension_semantics=("arbitrary",), collective_id=0, has_side_effects=True, vmem_limit_bytes=VMEM_LIMIT),
        )(tokens, keymask, cols, norm_attn.reshape(1, d_model), wqkv, wo, norm_moe.reshape(1, d_model), w_gate)

        tile = all_rows // 2
        ret = pl.pallas_call(
            functools.partial(expert_kernel, tile=tile),
            name="experts",
            grid=(e_loc,),
            in_specs=[
                pl.BlockSpec((1, all_rows, d_model), lambda i: (i, 0, 0)),
                pl.BlockSpec((1, d_model, ff), lambda i: (i, 0, 0)),
                pl.BlockSpec((1, ff, d_model), lambda i: (i, 0, 0)),
            ],
            out_specs=anywhere,
            out_shape=jax.ShapeDtypeStruct((experts, steps * rows, d_model), BF16),
            scratch_shapes=[
                pltpu.VMEM((tile, ff), BF16),
                pltpu.VMEM((e_loc, all_rows, d_model), BF16),
                pltpu.SemaphoreType.DMA,
                pltpu.SemaphoreType.DMA,
                pltpu.SemaphoreType.DMA,
            ],
            compiler_params=pltpu.CompilerParams(
                dimension_semantics=("arbitrary",), collective_id=1, has_side_effects=True, vmem_limit_bytes=VMEM_LIMIT),
        )(recv, w_in, w_out)

        out, aux = pl.pallas_call(
            functools.partial(back_kernel, n_groups=groups * N_DEV),
            name="back",
            grid=(steps,),
            in_specs=[
                pl.BlockSpec((experts, rows, d_model), lambda i: (0, i, 0)),
                pl.BlockSpec((2, seq, d_model), lambda i: (i, 0, 0)),
                pl.BlockSpec((2, seq, experts), lambda i: (i, 0, 0)),
                pl.BlockSpec((N_DEV, 8, experts), lambda i: (0, 0, 0)),
            ],
            out_specs=[
                pl.BlockSpec((2, seq, d_model), lambda i: (i, 0, 0)),
                pl.BlockSpec((8, experts), lambda i: (0, 0)),
            ],
            out_shape=[
                jax.ShapeDtypeStruct((groups, seq, d_model), BF16),
                jax.ShapeDtypeStruct((8, experts), F32),
            ],
            compiler_params=pltpu.CompilerParams(dimension_semantics=("arbitrary",), vmem_limit_bytes=VMEM_LIMIT),
        )(ret, hidden, meta, auxr)
        return out, aux[0, 0]

    by_group = P("ep")
    replicated = P()
    in_specs = (by_group, by_group, by_group, by_group, replicated, replicated, replicated, replicated, replicated, replicated, replicated, by_group, by_group)
    return jax.shard_map(local_step, mesh=mesh, in_specs=in_specs, out_specs=(by_group, replicated), check_vma=False)
```

time: 668 us -> 352 us (0.53); the launches traced: 656 us -> 351 us
  Pallas kernels: 0 us -> 333 us
  blocking collectives: 328 us -> 0 us
  matrix products: 193 us -> 0 us
  other arithmetic: 68.1 us -> 4.74 us
  local copies, waits for them, and re-layouts: 57 us -> 12.6 us
    pallas_call x0 -> x3, Pallas kernels: none -> 333 us  [the longest x1 161 us: local_step(): pl.pallas_call(functools.partial(front_kernel, heads=heads, head_dim=head...]
    dot_general x8 -> x0, matrix products: 193 us -> none  [the longest x1 49.1 us: local_step(): jnp.einsum('egcd,edf->egcf', received, w_in, preferred_element_type=jnp.f...]
    psum x1 -> x0, blocking collectives: 181 us -> none  [local_step(): aux_loss = lax.psum(aux_sum, 'ep') * experts / (groups_local * n_dev)]
    all_to_all x1 -> x0, blocking collectives: 147 us -> none  [local_step(): received = lax.all_to_all(send_buf, 'ep', 0, 1, tiled=True)]
    sub x3 -> x0, other arithmetic: 53.4 us -> none  [the longest x1 50.5 us: attention_block(): attn_probs = jax.nn.softmax(scores, axis=-1).astype(jnp.bfloat16)]
    convert_element_type x2 -> x0, local copies, waits for them, and re-layouts: 39 us -> none  [the longest x1 21.4 us: local_step(): jnp.einsum('gsec,gsd->egcd', dispatch, moe_in, preferred_element_type=jnp...]
    all_to_all x2 -> x0, local copies, waits for them, and re-layouts: 8.83 us -> none  [local_step(): received = lax.all_to_all(send_buf, 'ep', 0, 1, tiled=True)]
    reshape x0 -> x6, local copies, waits for them, and re-layouts: none -> 8.6 us  [the longest x3 4.71 us: local_step(): w.reshape(d_model, hw)]
  transfers between devices with their start and end apart: 1 -> 0, of which waited for: 0 -> 0; matrix products, arithmetic and copies ran while one was open for 0% -> 0% of each run, Pallas kernels for 0% -> 0%
where the time goes in v1:
time: 352 us; the launch traced here: 351 us
  Pallas kernels  333 us (95%)
  local copies, waits for them, and re-layouts  12.6 us (4%)
  other arithmetic  4.74 us (1%)
    pallas_call x1, Pallas kernels, local_step(): pl.pallas_call(functools.partial(front_kernel, heads=heads, head_dim=head...  161 us
    pallas_call x1, Pallas kernels, local_step(): pl.pallas_call(functools.partial(expert_kernel, tile=tile), name='experts...  156 us
    pallas_call x1, Pallas kernels, local_step(): pl.pallas_call(functools.partial(back_kernel, n_groups=groups * N_DEV), n...  15.8 us

profile of v1, /device:TPU:1, one launch (start us, length us, event | category | flops | bytes accessed | tf_op | source)
XLA Modules:
  0.0 350.8 jit_solution(14739856034834763804)
XLA Ops:
  0.6 1.3 reshape.26.norm_attn_ref
  1.9 1.3 reshape.31.norm_moe_ref
  3.2 0.7 convert_bitcast_fusion
  3.9 1.3 reshape.25.keymask_ref
  5.2 0.8 copy_convert_fusion
  6.0 1.3 pad_maximum_fusion.1
  7.3 1.6 copy.26
  8.9 1.6 copy.27
  10.5 1.6 copy.28
  12.1 1.9 pad_maximum_fusion.wqkv_ref
  14.0 2.8 copy.29.cols_ref
  16.8 161.3 %front.1 = (bf16[16,256,768]{2,1,0:T(8,128)(2,1)}, f32[16,256,128]{2,1,0:T(8,128)}, bf16[8,1024,768]{2,1,0:T(8,128)(2,1)}, f32[16,8,128]{2,1,0:T(8,128)}) custom-call(bf16[16,256,768]{2,1,0:T(8,128)(2,1)} %tokens_ref.1, s32[16,1,256]{2,1,0:T(1,128)} %reshape.25.keymask_ref, f32[16,256,4]{2,1,0:T(8,128)} %copy.29.cols_ref, f32[1,768]{1,0:T(1,128)} %reshape.26.norm_attn_ref, ...), custom_call_target="tpu_custom_call" | custom-call | tf_op jit(solution)/shard_map/front/pallas_call | solution.py:297
  178.2 155.7 %experts.1.ret_ref = bf16[128,64,768]{2,1,0:T(8,128)(2,1)} custom-call(bf16[8,1024,768]{2,1,0:T(8,128)(2,1)} %get-tuple-element.8.recv_ref, bf16[8,768,3072]{2,1,0:T(8,128)(2,1)} %w_in_ref.1, bf16[8,3072,768]{2,1,0:T(8,128)(2,1)} %w_out_ref.1), custom_call_target="tpu_custom_call" | custom-call | tf_op jit(solution)/shard_map/experts/pallas_call | solution.py:336
  333.9 15.8 %back.1 = (bf16[16,256,768]{2,1,0:T(8,128)(2,1)}, f32[8,128]{1,0:T(8,128)}) custom-call(bf16[128,64,768]{2,1,0:T(8,128)(2,1)} %experts.1.ret_ref, bf16[16,256,768]{2,1,0:T(8,128)(2,1)} %get-tuple-element.9.hidden_ref, f32[16,256,128]{2,1,0:T(8,128)} %get-tuple-element.10.meta_ref, f32[16,8,128]{2,1,0:T(8,128)} %get-tuple-element.11.auxr_ref), custom_call_target="tpu_custom_call" | custom-call | tf_op jit(solution)/shard_map/back/pallas_call | solution.py:358
  349.6 1.2 slice.3

commit v2 on v1

--- a/solution.py
+++ b/solution.py
@@ -38,10 +38,14 @@
     return jnp.dot(a, b, preferred_element_type=F32)
 
 
+def dot_nt(a, b):
+    return lax.dot_general(a, b, (((1,), (1,)), ((), ())), preferred_element_type=F32)
+
+
 def front_kernel(
-    tokens_ref, keymask_ref, cols_ref, norm_attn_ref, wqkv_ref, wo_ref, norm_moe_ref, wgate_ref,
+    tokens_ref, pad_ref, draw_ref, choices_ref, norm_attn_ref, wq_ref, wk_ref, wv_ref, wo_ref, norm_moe_ref, wgate_ref,
     hidden_ref, meta_ref, recv_ref, auxr_ref,
-    qkv_s, ctx_s, wg_s, aux_s, send_s, send_sem, recv_sem, local_sem, aux_send_sem, aux_recv_sem,
+    q_s, k_s, v_s, ctx_s, s_s, p_s, wg_s, aux_s, send_s, send_sem, recv_sem, local_sem, aux_send_sem, aux_recv_sem,
     *, heads, head_dim, capacity,
 ):
     step = pl.program_id(0)
@@ -72,14 +76,14 @@
     def _():
         greet(me)
         aux_s[...] = jnp.zeros_like(aux_s)
-        wg = wgate_ref[...]
+        wg = wgate_ref[...].T
         hi = wg.astype(BF16)
         rest = wg - hi.astype(F32)
         mid = rest.astype(BF16)
         low = (rest - mid.astype(F32)).astype(BF16)
-        wg_s[:, 0:experts] = hi
-        wg_s[:, experts:2 * experts] = mid
-        wg_s[:, 2 * experts:3 * experts] = low
+        wg_s[0:experts] = hi
+        wg_s[experts:2 * experts] = mid
+        wg_s[2 * experts:3 * experts] = low
 
     @pl.when(step == 1)
     def _():
@@ -90,72 +94,87 @@
         send_pair(step - 1)
 
     x = tokens_ref[...].reshape(2 * seq, d_model)
-    a = rms_norm(x.astype(F32), norm_attn_ref[...])
-    qkv_s[...] = dot(a, wqkv_ref[...]).astype(BF16)
+    a = rms_norm(x.astype(F32), norm_attn_ref[...][None, :])
+    q_s[...] = dot_nt(wq_ref[...], a).astype(BF16)
+    k_s[...] = dot_nt(a, wk_ref[...]).astype(BF16)
+    v_s[...] = dot_nt(wv_ref[...], a).astype(BF16)
 
     width = 2 * head_dim
     lane = lax.broadcasted_iota(jnp.int32, (1, width), 1)
-    ones = [(lane < head_dim).astype(F32).astype(BF16), (lane >= head_dim).astype(F32).astype(BF16)]
-    scaled = [m * jnp.asarray(head_dim ** -0.5, BF16) for m in ones]
-    hw = heads * head_dim
+    scale = head_dim ** -0.5
+    sides = [jnp.where(lane < head_dim, scale, 0.0).astype(BF16), jnp.where(lane < head_dim, 0.0, scale).astype(BF16)]
+    cut = seq // 2
+    late_key = lax.broadcasted_iota(jnp.int32, (seq - cut, 128), 0) + cut
+    batch = s_s.shape[1]
+    lanes = 128
+    buf = 0
     for grp in range(2):
         tok = pl.ds(grp * seq, seq)
-        keep_key = keymask_ref[grp] == 1
-        for pair_idx in range(heads // 2):
-            off = pair_idx * width
-            q = qkv_s[tok, pl.ds(off, width)]
-            k = qkv_s[tok, pl.ds(hw + off, width)]
-            v = qkv_s[tok, pl.ds(2 * hw + off, width)]
-            ctx = None
-            for side in range(2):
-                s = lax.dot_general(q * scaled[side], k, (((1,), (1,)), ((), ())), preferred_element_type=F32)
-                s = jnp.where(keep_key, s, -1e30)
-                ex = jnp.exp(s - jnp.max(s, axis=-1, keepdims=True))
-                prob = (ex * (1.0 / jnp.sum(ex, axis=-1, keepdims=True))).astype(BF16)
-                part = dot(prob, v * ones[side])
-                ctx = part if ctx is None else ctx + part
-            ctx_s[tok, pl.ds(off, width)] = ctx.astype(BF16)
-
-    hidden = (x.astype(F32) + dot(ctx_s[...], wo_ref[...])).astype(BF16)
+        length = jnp.sum(pad_ref[pl.ds(2 * step + grp, 1), :], axis=1, keepdims=True)
+        keep_late = late_key < length
+        for first in range(0, heads, batch):
+            for i in range(batch):
+                off = (first + i) // 2 * width
+                k = k_s[tok, pl.ds(off, width)] * sides[(first + i) % 2]
+                s_s[buf, i] = dot(k, q_s[pl.ds(off, width), tok])
+            for i in range(batch):
+                for col in range(0, seq, lanes):
+                    cols = pl.ds(col, lanes)
+                    early = s_s[buf, i, pl.ds(0, cut), cols]
+                    late = jnp.where(keep_late, s_s[buf, i, pl.ds(cut, seq - cut), cols], -1e30)
+                    top = jnp.maximum(jnp.max(early, axis=0, keepdims=True), jnp.max(late, axis=0, keepdims=True))
+                    early = jnp.exp(early - top)
+                    late = jnp.exp(late - top)
+                    inv = 1.0 / (jnp.sum(early, axis=0, keepdims=True) + jnp.sum(late, axis=0, keepdims=True))
+                    p_s[buf, i, pl.ds(0, cut), cols] = (early * inv).astype(BF16)
+                    p_s[buf, i, pl.ds(cut, seq - cut), cols] = (late * inv).astype(BF16)
+            for i in range(batch):
+                head = pl.ds((first + i) * head_dim, head_dim)
+                ctx_s[head, tok] = dot(v_s[head, tok], p_s[buf, i]).astype(BF16)
+            buf = 1 - buf
+
+    attn = lax.dot_general(ctx_s[...], wo_ref[...], (((0,), (0,)), ((), ())), preferred_element_type=F32)
+    hidden = (x.astype(F32) + attn).astype(BF16)
     hidden_ref[...] = hidden.reshape(2, seq, d_model)
-    b = rms_norm(hidden.astype(F32), norm_moe_ref[...])
-    lg = dot(b, wg_s[...])
-    logits = (lg[:, 2 * experts:] + lg[:, experts:2 * experts]) + lg[:, :experts]
-    ex = jnp.exp(logits - jnp.max(logits, axis=-1, keepdims=True))
-    gate_probs = ex / jnp.sum(ex, axis=-1, keepdims=True)
-
-    eid = lax.broadcasted_iota(jnp.int32, (seq, experts), 1)
-    tri = (lax.broadcasted_iota(jnp.int32, (seq, seq), 0) >= lax.broadcasted_iota(jnp.int32, (seq, seq), 1)).astype(F32).astype(BF16)
-    slot_id = lax.broadcasted_iota(jnp.int32, (seq, slots), 1)
-    meta_lane = lax.broadcasted_iota(jnp.int32, (seq, experts), 1)
+    b = rms_norm(hidden.astype(F32), norm_moe_ref[...][None, :])
+    lg = dot_nt(wg_s[...], b)
+    logits = (lg[2 * experts:] + lg[experts:2 * experts]) + lg[:experts]
+    ex = jnp.exp(logits - jnp.max(logits, axis=0, keepdims=True))
+    gate_probs = ex / jnp.sum(ex, axis=0, keepdims=True)
+
+    eid = lax.broadcasted_iota(jnp.int32, (experts, seq), 0)
+    tri = jnp.where(lax.broadcasted_iota(jnp.int32, (seq, seq), 0) <= lax.broadcasted_iota(jnp.int32, (seq, seq), 1), 1.0, 0.0).astype(BF16)
+    slot_id = lax.broadcasted_iota(jnp.int32, (slots, seq), 0)
+    meta_row = lax.broadcasted_iota(jnp.int32, (8, seq), 0)
     picked = []
     for grp in range(2):
-        p = gate_probs[grp * seq:(grp + 1) * seq]
-        cols = cols_ref[grp]
-        valid = cols[:, 0:1] == 1.0
-        draw = cols[:, 1:2]
-        e1 = cols[:, 2:3].astype(jnp.int32)
-        e2 = cols[:, 3:4].astype(jnp.int32)
+        p = gate_probs[:, grp * seq:(grp + 1) * seq]
+        valid = pad_ref[pl.ds(2 * step + grp, 1), :] == 1
+        draw = draw_ref[pl.ds(2 * step + grp, 1), :]
+        e1 = choices_ref[grp, 0:1, :]
+        e2 = choices_ref[grp, 1:2, :]
         hot1 = eid == e1
         hot2 = eid == e2
-        p1 = jnp.sum(jnp.where(hot1, p, 0.0), axis=-1, keepdims=True)
-        p2 = jnp.sum(jnp.where(hot2, p, 0.0), axis=-1, keepdims=True)
+        p1 = jnp.sum(jnp.where(hot1, p, 0.0), axis=0, keepdims=True)
+        p2 = jnp.sum(jnp.where(hot2, p, 0.0), axis=0, keepdims=True)
         g1 = p1 / (p1 + p2)
         g2 = p2 / (p1 + p2)
         want2 = valid & (draw < 2.0 * g2)
         take1 = jnp.where(hot1 & valid, 1.0, 0.0)
         take2 = jnp.where(hot2 & want2, 1.0, 0.0)
-        cum = dot(tri, jnp.concatenate([take1, take2], axis=1).astype(BF16))
-        cum1 = cum[:, :experts]
-        cum2 = cum[:, experts:]
-        count1 = cum1[seq - 1:seq, :]
-        pos1 = jnp.sum((cum1 - 1.0) * take1, axis=-1, keepdims=True).astype(jnp.int32)
-        pos2 = jnp.sum((cum2 - 1.0 + jnp.minimum(count1, float(capacity))) * take2, axis=-1, keepdims=True).astype(jnp.int32)
+        cum = dot(jnp.concatenate([take1, take2], axis=0).astype(BF16), tri)
+        cum1 = cum[:experts]
+        cum2 = cum[experts:]
+        count1 = cum1[:, seq - 1:seq]
+        pos1 = jnp.sum((cum1 - 1.0) * take1, axis=0, keepdims=True).astype(jnp.int32)
+        pos2 = jnp.sum((cum2 - 1.0 + jnp.minimum(count1, float(capacity))) * take2, axis=0, keepdims=True).astype(jnp.int32)
         keep1 = valid & (pos1 < capacity)
         keep2 = want2 & (pos2 < capacity)
 
-        density = jnp.sum(jnp.where(valid, p, 0.0), axis=0, keepdims=True) / seq
-        aux_s[0:1, :] += count1 / seq * density
+        share = jnp.where(valid, p, 0.0) * (count1 * (1.0 / (seq * seq)))
+        share = jnp.sum(share.reshape(experts // 8, 8, seq), axis=0)
+        for col in range(seq // 128):
+            aux_s[...] += share[:, col * 128:(col + 1) * 128]
 
         def places(e, pos, keep):
             dev = e // e_loc
@@ -169,13 +188,13 @@
 
         d1, c1 = places(e1, pos1, keep1)
         d2, c2 = places(e2, pos2, keep2)
-        meta = jnp.where(meta_lane == 0, c1.astype(F32), 0.0)
-        meta = jnp.where(meta_lane == 1, c2.astype(F32), meta)
-        meta = jnp.where(meta_lane == 2, g1, meta)
-        meta = jnp.where(meta_lane == 3, g2, meta)
+        meta = jnp.where(meta_row == 0, c1.astype(F32), 0.0)
+        meta = jnp.where(meta_row == 1, c2.astype(F32), meta)
+        meta = jnp.where(meta_row == 2, g1, meta)
+        meta = jnp.where(meta_row == 3, g2, meta)
         meta_ref[grp] = meta
         disp_mat = jnp.where((slot_id == d1) | (slot_id == d2), 1.0, 0.0).astype(BF16)
-        got = lax.dot_general(disp_mat, b[grp * seq:(grp + 1) * seq], (((0,), (0,)), ((), ())), preferred_element_type=F32)
+        got = dot(disp_mat, b[grp * seq:(grp + 1) * seq])
         picked.append(got.reshape(N_DEV * half, rows, d_model))
 
     top = lax.broadcasted_iota(jnp.int32, (1, rows, 1), 1) < capacity
@@ -257,7 +276,7 @@
     z = ret_ref[...].reshape(experts * rows, d_model)
     slot_id = lax.broadcasted_iota(jnp.int32, (seq, experts * rows), 1)
     for grp in range(2):
-        meta = meta_ref[grp]
+        meta = meta_ref[grp].T
         c1 = meta[:, 0:1].astype(jnp.int32)
         c2 = meta[:, 1:2].astype(jnp.int32)
         comb = jnp.where(slot_id == c1, meta[:, 2:3], 0.0) + jnp.where(slot_id == c2, meta[:, 3:4], 0.0)
@@ -284,11 +303,8 @@
         steps = groups // 2
         all_rows = N_DEV * steps * rows
 
-        wqkv = jnp.concatenate([w.reshape(d_model, hw) for w in (w_query, w_key, w_value)], axis=1)
+        wq, wk, wv = (w.transpose(1, 2, 0).reshape(hw, d_model) for w in (w_query, w_key, w_value))
         wo = w_attn_out.reshape(hw, d_model)
-        cols = jnp.concatenate([
-            pad_mask.astype(F32)[:, :, None], second_draw[:, :, None], choices.astype(F32)], axis=-1)
-        keymask = pad_mask.reshape(groups, 1, seq)
 
         def whole(shape):
             return pl.BlockSpec(shape, lambda i: (0,) * len(shape), pipeline_mode=pl.Buffered(1))
@@ -300,27 +316,31 @@
             grid=(steps,),
             in_specs=[
                 pl.BlockSpec((2, seq, d_model), lambda i: (i, 0, 0)),
-                pl.BlockSpec((2, 1, seq), lambda i: (i, 0, 0)),
-                pl.BlockSpec((2, seq, 4), lambda i: (i, 0, 0)),
-                whole((1, d_model)), whole((d_model, 3 * hw)), whole((hw, d_model)),
-                whole((1, d_model)), whole((d_model, experts)),
+                whole((groups, seq)), whole((groups, seq)),
+                pl.BlockSpec((2, 2, seq), lambda i: (i, 0, 0)),
+                whole((d_model,)), whole((hw, d_model)), whole((hw, d_model)), whole((hw, d_model)), whole((hw, d_model)),
+                whole((d_model,)), whole((d_model, experts)),
             ],
             out_specs=[
                 pl.BlockSpec((2, seq, d_model), lambda i: (i, 0, 0)),
-                pl.BlockSpec((2, seq, experts), lambda i: (i, 0, 0)),
+                pl.BlockSpec((2, 8, seq), lambda i: (i, 0, 0)),
                 anywhere, anywhere,
             ],
             out_shape=[
                 jax.ShapeDtypeStruct((groups, seq, d_model), BF16),
-                jax.ShapeDtypeStruct((groups, seq, experts), F32),
+                jax.ShapeDtypeStruct((groups, 8, seq), F32),
                 jax.ShapeDtypeStruct((e_loc, all_rows, d_model), BF16),
-                jax.ShapeDtypeStruct((N_DEV, 8, experts), F32),
+                jax.ShapeDtypeStruct((N_DEV, 8, 128), F32),
             ],
             scratch_shapes=[
-                pltpu.VMEM((2 * seq, 3 * hw), BF16),
+                pltpu.VMEM((hw, 2 * seq), BF16),
                 pltpu.VMEM((2 * seq, hw), BF16),
-                pltpu.VMEM((d_model, 3 * experts), BF16),
-                pltpu.VMEM((8, experts), F32),
+                pltpu.VMEM((hw, 2 * seq), BF16),
+                pltpu.VMEM((hw, 2 * seq), BF16),
+                pltpu.VMEM((2, 4, seq, seq), F32),
+                pltpu.VMEM((2, 4, seq, seq), BF16),
+                pltpu.VMEM((3 * experts, d_model), BF16),
+                pltpu.VMEM((8, 128), F32),
                 pltpu.VMEM((steps, N_DEV, e_loc, rows, d_model), BF16),
                 pltpu.SemaphoreType.DMA,
                 pltpu.SemaphoreType.DMA,
@@ -330,7 +350,7 @@
             ],
             compiler_params=pltpu.CompilerParams(
                 dimension_semantics=("arbitrary",), collective_id=0, has_side_effects=True, vmem_limit_bytes=VMEM_LIMIT),
-        )(tokens, keymask, cols, norm_attn.reshape(1, d_model), wqkv, wo, norm_moe.reshape(1, d_model), w_gate)
+        )(tokens, pad_mask, second_draw, choices.transpose(0, 2, 1), norm_attn, wq, wk, wv, wo, norm_moe, w_gate)
 
         tile = all_rows // 2
         ret = pl.pallas_call(
@@ -362,16 +382,16 @@
             in_specs=[
                 pl.BlockSpec((experts, rows, d_model), lambda i: (0, i, 0)),
                 pl.BlockSpec((2, seq, d_model), lambda i: (i, 0, 0)),
-                pl.BlockSpec((2, seq, experts), lambda i: (i, 0, 0)),
-                pl.BlockSpec((N_DEV, 8, experts), lambda i: (0, 0, 0)),
+                pl.BlockSpec((2, 8, seq), lambda i: (i, 0, 0)),
+                pl.BlockSpec((N_DEV, 8, 128), lambda i: (0, 0, 0)),
             ],
             out_specs=[
                 pl.BlockSpec((2, seq, d_model), lambda i: (i, 0, 0)),
-                pl.BlockSpec((8, experts), lambda i: (0, 0)),
+                pl.BlockSpec((8, 128), lambda i: (0, 0)),
             ],
             out_shape=[
                 jax.ShapeDtypeStruct((groups, seq, d_model), BF16),
-                jax.ShapeDtypeStruct((8, experts), F32),
+                jax.ShapeDtypeStruct((8, 128), F32),
             ],
             compiler_params=pltpu.CompilerParams(dimension_semantics=("arbitrary",), vmem_limit_bytes=VMEM_LIMIT),
         )(ret, hidden, meta, auxr)

time: 352 us -> 331 us (0.940)
  local copies, waits for them, and re-layouts: 12.6 us -> 1.19 us
  Pallas kernels: 333 us -> 328 us
  other arithmetic: 4.74 us -> 0 us
    reshape x6 -> x0, local copies, waits for them, and re-layouts: 8.6 us -> none  [the longest x3 4.71 us: local_step(): w.reshape(d_model, hw)]
where the time goes in v2:
time: 331 us; the launch traced here: 330 us
  Pallas kernels  328 us (99%)
    pallas_call x1, Pallas kernels, local_step(): pl.pallas_call(functools.partial(front_kernel, heads=heads, head_dim=head...  158 us
    pallas_call x1, Pallas kernels, local_step(): pl.pallas_call(functools.partial(expert_kernel, tile=tile), name='experts...  154 us
    pallas_call x1, Pallas kernels, local_step(): pl.pallas_call(functools.partial(back_kernel, n_groups=groups * N_DEV), n...  15.6 us

profile of v2, /device:TPU:1, one launch (start us, length us, event | category | flops | bytes accessed | tf_op | source)
XLA Modules:
  0.0 329.7 jit_solution(10864184444722370976)
XLA Ops:
  0.6 157.9 %front.1 = (bf16[16,256,768]{2,1,0:T(8,128)(2,1)}, f32[16,8,256]{2,1,0:T(8,128)}, bf16[8,1024,768]{2,1,0:T(8,128)(2,1)}, f32[16,8,128]{2,1,0:T(8,128)}) custom-call(bf16[16,256,768]{2,1,0:T(8,128)(2,1)} %tokens_ref.1, s32[16,256]{1,0:T(8,128)} %pad_ref.1, f32[16,256]{1,0:T(8,128)} %draw_ref.1, s32[16,2,256]{2,1,0:T(2,128)} %bitcast.16, f32[768]{0:T(1024)} %norm_attn_ref.1, ...), custom_call_target="tpu_custom_call" | custom-call | tf_op jit(solution)/shard_map/front/pallas_call | solution.py:313
  158.5 154.4 %experts.1.ret_ref = bf16[128,64,768]{2,1,0:T(8,128)(2,1)} custom-call(bf16[8,1024,768]{2,1,0:T(8,128)(2,1)} %get-tuple-element.8.recv_ref, bf16[8,768,3072]{2,1,0:T(8,128)(2,1)} %w_in_ref.1, bf16[8,3072,768]{2,1,0:T(8,128)(2,1)} %w_out_ref.1), custom_call_target="tpu_custom_call" | custom-call | tf_op jit(solution)/shard_map/experts/pallas_call | solution.py:356
  312.9 15.6 %back.1 = (bf16[16,256,768]{2,1,0:T(8,128)(2,1)}, f32[8,128]{1,0:T(8,128)}) custom-call(bf16[128,64,768]{2,1,0:T(8,128)(2,1)} %experts.1.ret_ref, bf16[16,256,768]{2,1,0:T(8,128)(2,1)} %get-tuple-element.9.hidden_ref, f32[16,8,256]{2,1,0:T(8,128)} %get-tuple-element.10.meta_ref, f32[16,8,128]{2,1,0:T(8,128)} %get-tuple-element.11.auxr_ref), custom_call_target="tpu_custom_call" | custom-call | tf_op jit(solution)/shard_map/back/pallas_call | solution.py:378
  328.5 1.2 slice.3
